TPU v7x, 32 devices: a 4x4x1 block of a 4x4x8 slice. The times are simulated.
32 devices in a mesh: dp: 1 (over z), tp: 32 (over y, x, core).
Axes of the slice: x: 4, y: 4, z: 1, core: 2. Of those that a mesh axis runs over, the one named last changes fastest.
The devices are a block of a 4x4x8 slice.
Arguments:
- x_a: bfloat16 [4096, 2048], P(('dp', 'tp'))
- x_b: bfloat16 [4096, 2048], P(('dp', 'tp'))
- labels_a: int32 [4096], P(('dp', 'tp'))
- labels_b: int32 [4096], P(('dp', 'tp'))
- w_head: bfloat16 [2048, 49152], P(None, 'tp')
Outputs:
- output 1: float32 [2], P('dp')
- output 2: bfloat16 [2048, 49152], P('dp', 'tp')
- output 3: bfloat16 [4096, 2048], P(('dp', 'tp'))
- output 4: bfloat16 [4096, 2048], P(('dp', 'tp'))
All inputs are finite; a program needn't handle non-finite values.
Results may differ from a plain program's by a relative error of at most 0.001.
Values are sent between devices in bfloat16 or wider.
A program may use at most 768 MiB of HBM per device.

v0:
```python
import jax
import jax.numpy as jnp
from jax import lax
from jax.sharding import PartitionSpec as P


def solution(mesh):
    group_size = mesh.shape["tp"]

    def local_step(x_a, x_b, labels_a, labels_b, w_local):
        tok_rows = x_a.shape[0]
        shard_cols = w_local.shape[1]
        tokens = tok_rows * group_size
        x_full = lax.all_gather(jnp.stack([x_a, x_b]), "tp", axis=1, tiled=True)
        label_full = lax.all_gather(jnp.stack([labels_a, labels_b]), "tp", axis=1, tiled=True)
        logits = jnp.einsum("mth,hv->mtv", x_full, w_local, preferred_element_type=jnp.float32)
        col_ids = lax.broadcasted_iota(jnp.int32, (1, 1, shard_cols), 2) + lax.axis_index("tp") * shard_cols
        label_hit = col_ids == label_full[..., None]
        local_target = jnp.sum(jnp.where(label_hit, logits, 0.0), axis=-1)
        row_max = lax.pmax(jnp.max(logits, axis=-1), "tp")
        shifted = jnp.exp(logits - row_max[..., None])
        stat_sums = lax.psum(jnp.stack([jnp.sum(shifted, axis=-1), local_target]), "tp")
        row_sum = stat_sums[0]
        loss_tok = row_max + jnp.log(row_sum) - stat_sums[1]
        losses = jnp.mean(loss_tok, axis=-1)
        grad_logits = ((shifted / row_sum[..., None] - label_hit.astype(jnp.float32)) / tokens).astype(jnp.bfloat16)
        grad_w = jnp.einsum("mth,mtv->hv", x_full, grad_logits, preferred_element_type=jnp.float32).astype(jnp.bfloat16)
        grad_part = jnp.einsum("mtv,hv->mth", grad_logits, w_local, preferred_element_type=jnp.float32)
        grad_x = lax.psum_scatter(grad_part, "tp", scatter_dimension=1, tiled=True).astype(jnp.bfloat16)
        return losses, grad_w, grad_x[0], grad_x[1]

    row_spec = P(("dp", "tp"), None)
    label_spec = P(("dp", "tp"))
    return jax.shard_map(local_step, mesh=mesh, in_specs=(row_spec, row_spec, label_spec, label_spec, P(None, "tp")), out_specs=(P("dp"), P("dp", "tp"), row_spec, row_spec), check_vma=False)
```

profile of v0, /device:TPU:97, one launch (start us, length us, event | category | flops | bytes accessed | tf_op | source)
XLA Modules:
  0.0 722.5 jit_solution(12889838077995197136)
XLA Ops:
  7.2 0.1 all-gather.2.cloned.1.call-start
  7.2 2.3 pad_maximum_fusion
  9.5 0.1 all-gather.2.cloned.1.call-update
  9.6 0.1 all-reduce.2.cloned.1.call-start
  9.7 0.7 pad_add_fusion
  10.3 32.6 %all_gather.7 = s32[2,4096]{1,0:T(2,128)S(1)} all-gather(s32[2,128]{1,0:T(2,128)S(1)} %pad_add_fusion), channel_id=1, replica_groups=mesh['dp'=1,'tp'=32] {'tp'}, dimensions={1}, use_global_device_ids=true | all-gather | bytes 33792 | tf_op jit(solution)/shard_map/all_gather | solution.py:15
  43.0 80.4 %all-gather.2.cloned.1.call-done = bf16[2,4096,2048]{2,1,0:T(8,128)(2,1)} async-done(((bf16[2,128,2048]{2,1,0:T(8,128)(2,1)}), bf16[2,4096,2048]{2,1,0:T(8,128)(2,1)}) %all-gather.2.cloned.1.call-update) | async-done | bytes 33554448 | tf_op jit(solution)/shard_map/all_gather | solution.py:14
  123.4 60.8 %fusion.11 = (f32[2,4096]{1,0:T(2,128)S(1)}, f32[2,4096,1536]{1,2,0:T(8,128)}) fusion(bf16[2,4096,2048]{2,1,0:T(8,128)(2,1)} %all-gather.2.cloned.1.call-done, bf16[2048,1536]{1,0:T(8,128)(2,1)} %param.9), kind=kOutput, calls=%fused_computation.24 | convolution fusion | flops 51552182272 | bytes 90210304 | tf_op jit(solution)/shard_map/mth,hv->mtv/dot_general | solution.py:16
  184.2 44.8 %pmax.7 = f32[2,4096]{1,0:T(2,128)S(1)} all-reduce(f32[2,4096]{1,0:T(2,128)S(1)} %get-tuple-element.8), channel_id=1, replica_groups=mesh['dp'=1,'tp'=32] {'tp'}, use_global_device_ids=true, to_apply=%region_1.2 | all-reduce | flops 8192 | bytes 65536 | tf_op jit(solution)/shard_map/pmax | solution.py:20
  229.0 22.0 %fusion.4 = (f32[2,4096]{1,0:T(2,128)S(1)}, f32[2,4096]{1,0:T(2,128)S(1)}) fusion(f32[2,4096,1536]{1,2,0:T(8,128)} %get-tuple-element.9, f32[2,4096]{1,0:T(2,128)S(1)} %pmax.7, s32[2,4096]{1,0:T(2,128)S(1)} %all_gather.7, s32[1536]{0:T(1024)S(1)} %iota_add_fusion), kind=kLoop, calls=%fused_computation.7 | loop fusion | flops 62898176 | bytes 50468864 | tf_op jit(solution)/shard_map/reduce_sum | solution.py:22
  251.0 0.7 pad_maximum_fusion.1
  251.7 0.1 all-reduce.2.cloned.1.call-update
  251.7 0.2 reduce-scatter.2.cloned.1.call-start
  252.0 89.5 %all-reduce.2.cloned.1.call-done = f32[2,2,4096]{2,1,0:T(2,128)} async-done(((f32[2,2,4096]{2,1,0:T(2,128)}), f32[2,2,4096]{2,1,0:T(2,128)}) %all-reduce.2.cloned.1.call-update) | async-done | bytes 65552 | tf_op jit(solution)/shard_map/psum | solution.py:22
  341.4 0.8 slice_bitcast_fusion.3
  342.2 25.7 %fusion.3 = bf16[2,4096,1536]{1,2,0:T(8,128)(2,1)} fusion(f32[2,4096,1536]{1,2,0:T(8,128)} %get-tuple-element.9, f32[2,4096]{1,0:T(2,128)S(1)} %slice_bitcast_fusion.3, s32[2,4096]{1,0:T(2,128)S(1)} %all_gather.7, f32[2,4096]{1,0:T(2,128)S(1)} %pmax.7, s32[1536]{0:T(1024)S(1)} %iota_add_fusion), kind=kLoop, calls=%fused_computation.5 | loop fusion | flops 88080384 | bytes 75601920 | tf_op jit(solution)/shard_map/convert_element_type | solution.py:26
  367.9 60.7 %fusion.5 = f32[2,4096,2048]{2,1,0:T(8,128)} fusion(bf16[2,4096,1536]{1,2,0:T(8,128)(2,1)} %fusion.3, bf16[2048,1536]{1,0:T(8,128)(2,1)} %param.9), kind=kOutput, calls=%fused_computation.9 | convolution fusion | flops 51539607552 | bytes 98566144 | tf_op jit(solution)/shard_map/mtv,hv->mth/dot_general | solution.py:28
  428.7 0.8 copy-done
  429.5 0.2 fusion.10
  429.6 0.5 broadcast_multiply_fusion
  430.1 60.6 %bitcast_convert_fusion = bf16[2048,1536]{1,0:T(8,128)(2,1)} fusion(bf16[2,4096,2048]{2,1,0:T(8,128)(2,1)} %all-gather.2.cloned.1.call-done, bf16[2,4096,1536]{1,2,0:T(8,128)(2,1)} %fusion.3), kind=kOutput, calls=%fused_computation.8 | convolution fusion | flops 51542753280 | bytes 65011712 | tf_op jit(solution)/shard_map/mth,mtv->hv/dot_general | solution.py:27
  490.7 222.5 %reduce-scatter.2.cloned.1.call-done = f32[2,128,2048]{2,1,0:T(8,128)} async-done(((f32[2,4096,2048]{2,1,0:T(8,128)}), f32[2,128,2048]{2,1,0:T(8,128)}) %reduce-scatter.2.cloned.1.call-update) | async-done | bytes 2097168 | tf_op jit(solution)/shard_map/reduce_scatter | solution.py:29
  713.1 1.7 convert_element_type.15
  714.9 1.0 slice_bitcast_fusion
  (3 shorter events, 0.1 us)
Async XLA Ops:
  7.2 116.2 %all-gather.2.cloned.1.call-start = ((), (), s32[]{:S(2)}) async-start(), calls=%async_computation.1 | async-start | bytes 34603008 | tf_op jit(solution)/shard_map/all_gather | solution.py:14
  9.6 331.9 %all-reduce.2.cloned.1.call-start = ((), (), s32[]{:S(2)}) async-start(), calls=%async_computation.2 | async-start | bytes 131072 | tf_op jit(solution)/shard_map/psum | solution.py:22
  251.7 461.4 %reduce-scatter.2.cloned.1.call-start = ((), (), s32[]{:S(2)}) async-start(), calls=%async_computation.3 | async-start | bytes 69206016 | tf_op jit(solution)/shard_map/reduce_scatter | solution.py:29
  428.6 0.8 copy-start
Sparse Core Ops, SparseCore 0:
  10.7 112.6 all-gather.1
  251.9 89.5 all-reduce.1
  428.8 284.2 reduce-scatter.1
where the time goes:
time: 723 us; the launch traced here: 722 us
  waiting for transfers between devices  392 us (54%)
  matrix products  182 us (25%)
  blocking collectives  77.5 us (11%)
  other arithmetic  53.7 us (7%)
  between operations  13.8 us (2%)
    reduce_scatter x1, waiting for transfers between devices, local_step(): lax.psum_scatter(grad_part, 'tp', scatter_dimension=1, tiled=True)  222 us
    psum x1, waiting for transfers between devices, local_step(): lax.psum(jnp.stack([jnp.sum(shifted, axis=-1), local_target]), 'tp')  89.5 us
    all_gather x1, waiting for transfers between devices, local_step(): x_full = lax.all_gather(jnp.stack([x_a, x_b]), 'tp', axis=1, tiled=True)  80.4 us
    dot_general x1, matrix products, local_step(): jnp.einsum('mth,hv->mtv', x_full, w_local, preferred_element_type=jnp.flo...  60.8 us
    dot_general x1, matrix products, local_step(): jnp.einsum('mtv,hv->mth', grad_logits, w_local, preferred_element_type=jn...  60.7 us
    dot_general x1, matrix products, local_step(): jnp.einsum('mth,mtv->hv', x_full, grad_logits, preferred_element_type=jnp...  60.6 us
    pmax x1, blocking collectives, local_step(): row_max = lax.pmax(jnp.max(logits, axis=-1), 'tp')  44.8 us
    all_gather x1, blocking collectives, local_step(): lax.all_gather(jnp.stack([labels_a, labels_b]), 'tp', axis=1, tiled=True)  32.6 us
  transfers between devices with their start and end apart: 3, of which 3 were waited for; matrix products, arithmetic and copies ran while one was open for 9% of the time, Pallas kernels for 0%

commit v1 on v0

v1 whole, which is shorter than its diff:
```python
import functools
import math

import jax
import jax.numpy as jnp
from jax import lax
from jax.experimental import pallas as pl
from jax.experimental.pallas import tpu as pltpu
from jax.sharding import PartitionSpec as P

MESH = pl.DeviceIdType.MESH
F32 = jnp.float32
BF16 = jnp.bfloat16
RINGS = 4
BLOCKS = 4
HALF = 3
PIECES = 2 * HALF
MBLOCKS = 8
BUFS = 3


def head_kernel(group, xa, xb, la, lb, w, loss, dw, dxa, dxb, e_hbm, xt_hbm,
                wv, xg, stage, xts, xtb, buf, dwr, dwb, dxo, m_store, s_store, t_store, labc,
                lab_in, st_out, st_in, bc_in, bc_out, ls_out, ls_in,
                x_sem, w_sem, wp_sem, lab_sem, ag_send, ag_recv, e_sem, xt_sem, xtr_sem, st_send, st_recv,
                bc_send, bc_recv, ls_sem, rs_send, rs_recv, credit, dw_send, dw_recv, dw_credit, dwo_sem, dxo_sem):
    chips = group // 2
    side = math.isqrt(chips)
    rows = xa.shape[0]
    slot_rows = 2 * rows
    rt = slot_rows // RINGS
    hb = xg.shape[2]
    pc = hb
    shard = w.shape[1]
    tokens = rows * group
    mb_rows = w.shape[0] // MBLOCKS
    lanes = lab_in.shape[2]

    me = lax.axis_index("tp")
    core = lax.rem(me, 2)
    chip = me // 2
    partner = me + 1 - 2 * core
    cx = lax.rem(chip, side)
    cy = chip // side
    diag = lax.rem(cx + cy, side)
    pos = (side * cy + diag, side * lax.rem(cx + 1, side) + diag)

    def dev(c):
        return {"tp": 2 * c + core}

    def chip_at(cycle, p):
        major, minor = p // side, lax.rem(p, side)
        if cycle == 0:
            yy = major
            xx = lax.rem(minor - major + side, side)
        else:
            xx = lax.rem(major + side - 1, side)
            yy = lax.rem(minor + 1 - major + side, side)
        return yy * side + xx

    def source(r, k):
        sign = -1 if r % 2 == 0 else 1
        return chip_at(r // 2, lax.rem(pos[r // 2] + sign * k + 2 * chips, chips))

    up = [source(r, 1) for r in range(RINGS)]
    down = [source(r, -1) for r in range(RINGS)]

    for b in range(BLOCKS):
        cols = pl.ds(b * hb, hb)
        pltpu.make_async_copy(xa.at[:, cols], xg.at[b, pl.ds(0, rows)], x_sem.at[2 * b]).start()
        pltpu.make_async_copy(xb.at[:, cols], xg.at[b, pl.ds(rows, rows)], x_sem.at[2 * b + 1]).start()
    pltpu.make_async_copy(w, wv.at[0], w_sem.at[0]).start()

    barrier = pltpu.get_barrier_semaphore()

    def hello(d, carry):
        pl.semaphore_signal(barrier, inc=1, device_id=dev(lax.rem(chip + d, chips)), device_id_type=MESH)
        return carry

    lax.fori_loop(1, chips, hello, 0)
    pl.semaphore_signal(barrier, inc=1, device_id={"tp": partner}, device_id_type=MESH)
    my_lab = lab_in.at[chip]
    my_lab[0:1, :] = la[...].astype(F32)
    my_lab[1:2, :] = lb[...].astype(F32)
    pl.semaphore_wait(barrier, chips)

    def ag_copy(k, j, r):
        src = xg.at[j, pl.ds(pl.multiple_of(k * slot_rows + r * rt, rt), rt)]
        dst = xg.at[j, pl.ds(pl.multiple_of((k + 1) * slot_rows + r * rt, rt), rt)]
        return pltpu.make_async_remote_copy(
            src_ref=src, dst_ref=dst, send_sem=ag_send.at[lax.rem(k, 4), j * RINGS + r],
            recv_sem=ag_recv.at[k + 1, j * RINGS + r], device_id=dev(down[r]), device_id_type=MESH)

    for b in range(BLOCKS):
        cols = pl.ds(b * hb, hb)
        pltpu.make_async_copy(xa.at[:, cols], xg.at[b, pl.ds(0, rows)], x_sem.at[2 * b]).wait()
        pltpu.make_async_copy(xb.at[:, cols], xg.at[b, pl.ds(rows, rows)], x_sem.at[2 * b + 1]).wait()
        for r in range(RINGS):
            ag_copy(0, b, r).start()

    w_swap = pltpu.make_async_remote_copy(
        src_ref=w, dst_ref=wv.at[1], send_sem=wp_sem.at[0], recv_sem=wp_sem.at[1],
        device_id={"tp": partner}, device_id_type=MESH)
    w_swap.start()

    def lab_copy(d):
        return pltpu.make_async_remote_copy(
            src_ref=lab_in.at[chip], dst_ref=lab_in.at[chip], send_sem=lab_sem.at[0, d], recv_sem=lab_sem.at[1, d],
            device_id=dev(lax.rem(chip + d, chips)), device_id_type=MESH)

    def lab_start(d, carry):
        lab_copy(d).start()
        return carry

    def lab_wait(d, carry):
        lab_copy(d).wait()
        return carry

    lax.fori_loop(1, chips, lab_start, 0)
    pltpu.make_async_copy(w, wv.at[0], w_sem.at[0]).wait()

    sub_i = lax.broadcasted_iota(jnp.int32, (rt, 128), 0)
    lane_i = lax.broadcasted_iota(jnp.int32, (rt, 128), 1)
    eye = sub_i == lane_i
    row_lane = lax.broadcasted_iota(jnp.int32, (1, 128), 1)
    lab_sub = lax.broadcasted_iota(jnp.int32, (rt, lanes), 0)
    lab_lane = lax.broadcasted_iota(jnp.int32, (rt, lanes), 1)
    piece_lane = lax.broadcasted_iota(jnp.int32, (slot_rows, 128), 1)

    def to_row(col):
        return jnp.sum(jnp.where(eye, col, 0.0), axis=0, keepdims=True)

    def to_col(row):
        return jnp.sum(jnp.where(eye, row, 0.0), axis=1, keepdims=True)

    def fill_labels(k):
        for r in range(RINGS):
            row = lab_in[source(r, k), r // 2:r // 2 + 1, :]
            col = jnp.sum(jnp.where(lab_lane == lab_sub + (r % 2) * rt, row, 0.0), axis=1, keepdims=True)
            labc[r * rt:(r + 1) * rt, :] = jnp.broadcast_to(col.astype(jnp.int32), (rt, 128))

    def base(lp):
        owner = me if lp < HALF else partner
        return owner * shard + (lp % HALF) * pc

    chunk = slot_rows // 8
    piece_iota = lax.broadcasted_iota(jnp.int32, (chunk, pc), 1)

    def z_piece(slot, lp):
        k0 = pl.multiple_of(slot * slot_rows, slot_rows)
        z = None
        for b in range(BLOCKS):
            part = jnp.dot(xg[b, pl.ds(k0, slot_rows), :],
                           wv[lp // HALF, b * hb:(b + 1) * hb, (lp % HALF) * pc:(lp % HALF + 1) * pc],
                           preferred_element_type=F32)
            z = part if z is None else z + part
        stage[lp] = z
        off = base(lp)
        for c in range(8):
            rs = slice(c * chunk, (c + 1) * chunk)
            zc = stage[lp, rs, :]
            m = jnp.max(zc, axis=1, keepdims=True)
            e = jnp.exp(zc - m)
            hit = piece_iota == labc[rs, 0:1] - off
            stage[lp, rs, :] = e
            m_store[pl.ds(pl.multiple_of(k0 + c * chunk, chunk), chunk), lp:lp + 1] = m
            s_store[rs, lp:lp + 1] = jnp.sum(e, axis=1, keepdims=True)
            t_store[rs, lp:lp + 1] = jnp.sum(jnp.where(hit, zc, 0.0), axis=1, keepdims=True)

    def e_write(slot, lp):
        return pltpu.make_async_copy(stage.at[lp], e_hbm.at[slot, lp], e_sem.at[lp])

    def xt_write(slot):
        return pltpu.make_async_copy(
            xts, xt_hbm.at[:, pl.ds(pl.multiple_of(slot * slot_rows, slot_rows), slot_rows)], xt_sem.at[0])

    def st_copy(slot, r):
        return pltpu.make_async_remote_copy(
            src_ref=st_out.at[slot, r], dst_ref=st_in.at[slot, r], send_sem=st_send.at[slot],
            recv_sem=st_recv.at[slot], device_id=dev(source(r, slot)), device_id_type=MESH)

    def poll(k, j):
        @pl.when(k < chips)
        def _():
            for r in range(RINGS):
                ag_copy(k - 1, j, r).wait_recv()

        @pl.when(k < chips - 1)
        def _():
            @pl.when(k >= 4)
            def _():
                for r in range(RINGS):
                    ag_copy(k - 4, j, r).wait_send()
            for r in range(RINGS):
                ag_copy(k, j, r).start()

    def gather_step(k, carry):
        slot = k - 1
        poll(k, 0)

        @pl.when(slot == 1)
        def _():
            lax.fori_loop(1, chips, lab_wait, 0)

        @pl.when(slot >= 1)
        def _():
            for lp in range(PIECES):
                e_write(slot - 1, lp).wait()
            xt_write(slot - 1).wait()

        fill_labels(slot)
        k0 = pl.multiple_of(slot * slot_rows, slot_rows)
        for blk in range(HALF):
            if blk == 1:
                @pl.when(slot == 0)
                def _():
                    w_swap.wait()
            for lp in (2 * blk, 2 * blk + 1):
                z_piece(slot, lp)
            for lp in (2 * blk, 2 * blk + 1):
                e_write(slot, lp).start()
            poll(k, blk + 1)
        for b in range(BLOCKS):
            xts[b * hb:(b + 1) * hb, :] = xg[b, pl.ds(k0, slot_rows), :].T
        xt_write(slot).start()

        valid = piece_lane < PIECES
        m_all = m_store[pl.ds(k0, slot_rows), :]
        m = jnp.max(jnp.where(valid, m_all, -jnp.inf), axis=1, keepdims=True)
        s = jnp.sum(jnp.where(valid, s_store[...] * jnp.exp(m_all - m), 0.0), axis=1, keepdims=True)
        t = jnp.sum(jnp.where(valid, t_store[...], 0.0), axis=1, keepdims=True)
        for r in range(RINGS):
            rs = slice(r * rt, (r + 1) * rt)
            tile = st_out.at[slot, r]
            tile[0:1, :] = to_row(m[rs])
            tile[1:2, :] = to_row(s[rs])
            tile[2:3, :] = to_row(t[rs])

        @pl.when(slot == 0)
        def _():
            for r in range(RINGS):
                st_in[0, r] = st_out[0, r]

        @pl.when(slot >= 1)
        def _():
            for r in range(RINGS):
                st_copy(slot, r).start()
        return carry

    lax.fori_loop(1, chips + 1, gather_step, 0)

    for lp in range(PIECES):
        e_write(chips - 1, lp).wait()

    def e_read(slot, lp):
        return pltpu.make_async_copy(e_hbm.at[slot, lp], stage.at[lp], e_sem.at[lp])

    for lp in range(PIECES):
        e_read(1, lp).start()
    xt_write(chips - 1).wait()

    def xt_read(mb):
        return pltpu.make_async_copy(
            xt_hbm.at[pl.ds(pl.multiple_of(mb * mb_rows, mb_rows), mb_rows), :], xtb.at[lax.rem(mb, 2)],
            xtr_sem.at[lax.rem(mb, 2)])

    xt_read(0).start()
    buf[0] = jnp.zeros(buf.shape[1:], F32)
    for k in range(chips - 5, chips - 1):
        for j in range(BLOCKS):
            for r in range(RINGS):
                ag_copy(k, j, r).wait_send()

    def st_wait(k, carry):
        pltpu.make_async_copy(st_in.at[k], st_in.at[k], st_recv.at[k]).wait()
        return carry

    lax.fori_loop(1, chips, st_wait, 0)
    inside = row_lane < rt
    parts = []
    for r in range(RINGS):
        m = st_in[0, r, 0:1, :]
        for k in range(1, chips):
            m = jnp.maximum(m, st_in[k, r, 0:1, :])
        s = jnp.zeros_like(m)
        t = jnp.zeros_like(m)
        for k in range(chips):
            s = s + st_in[k, r, 1:2, :] * jnp.exp(st_in[k, r, 0:1, :] - m)
            t = t + st_in[k, r, 2:3, :]
        bc_out[r:r + 1, :] = m
        bc_out[RINGS + r:RINGS + r + 1, :] = s
        parts.append(jnp.sum(jnp.where(inside, m + jnp.log(s) - t, 0.0), axis=1, keepdims=True))
    for mb in range(2):
        both = jnp.broadcast_to(parts[2 * mb] + parts[2 * mb + 1], (1, 128))
        bc_out[mb:mb + 1, :] = jnp.where(inside, bc_out[mb:mb + 1, :], both)
    bc_in[chip] = bc_out[...]

    def bc_copy(d):
        return pltpu.make_async_remote_copy(
            src_ref=bc_out, dst_ref=bc_in.at[chip], send_sem=bc_send.at[d], recv_sem=bc_recv.at[d],
            device_id=dev(lax.rem(chip + d, chips)), device_id_type=MESH)

    def bc_start(d, carry):
        bc_copy(d).start()
        return carry

    def bc_wait(d, carry):
        bc_copy(d).wait()
        return carry

    lax.fori_loop(1, chips, bc_start, 0)
    lax.fori_loop(1, chips, bc_wait, 0)

    def st_done(k, carry):
        pltpu.make_async_copy(st_out.at[k], st_out.at[k], st_send.at[k]).wait()
        return carry

    lax.fori_loop(1, chips, st_done, 0)
    total = bc_in[0]
    for c in range(1, chips):
        total = total + bc_in[c]
    ls_out[...] = total
    ls_copy = pltpu.make_async_remote_copy(
        src_ref=ls_out, dst_ref=ls_in, send_sem=ls_sem.at[0], recv_sem=ls_sem.at[1],
        device_id={"tp": partner}, device_id_type=MESH)
    ls_copy.start()

    def form_g(slot, prefetch):
        k0 = pl.multiple_of(slot * slot_rows, slot_rows)
        fill_labels(slot)
        m_cols = []
        inv_cols = []
        for r in range(RINGS):
            src = source(r, slot)
            m_cols.append(to_col(bc_in[src, r:r + 1, :]))
            inv_cols.append(1.0 / (to_col(bc_in[src, RINGS + r:RINGS + r + 1, :]) * tokens))
        for r in range(RINGS):
            rs = slice(r * rt, (r + 1) * rt)
            krs = pl.ds(pl.multiple_of(k0 + r * rt, rt), rt)
            s_store[rs, :] = jnp.exp(m_store[krs, :] - m_cols[r]) * inv_cols[r]
        for lp in range(PIECES):
            e_read(slot, lp).wait()
            off = base(lp)
            for c in range(8):
                rs = slice(c * chunk, (c + 1) * chunk)
                hit = piece_iota == labc[rs, 0:1] - off
                g = stage[lp, rs, :] * s_store[rs, lp:lp + 1] - jnp.where(hit, 1.0 / tokens, 0.0)
                xg[lp, pl.ds(pl.multiple_of(k0 + c * chunk, chunk), chunk), :] = g.astype(BF16)
            prefetch(lp)

    def start_next(slot):
        def go(lp):
            e_read(slot, lp).start()
        return go

    form_g(1, start_next(2))

    def rs_copy(s, j, r):
        b0, b1 = lax.rem(s, BUFS), lax.rem(s + 1, BUFS)
        return pltpu.make_async_remote_copy(
            src_ref=buf.at[b0, j, pl.ds(r * rt, rt)], dst_ref=buf.at[b1, j, pl.ds(r * rt, rt)],
            send_sem=rs_send.at[b0, j, r], recv_sem=rs_recv.at[b1, j, r],
            device_id=dev(down[r]), device_id_type=MESH)

    def dw_copy(mb, o):
        return pltpu.make_async_remote_copy(
            src_ref=stage.at[o], dst_ref=dwr.at[lax.rem(mb, 2), o], send_sem=dw_send.at[o],
            recv_sem=dw_recv.at[lax.rem(mb, 2), o], device_id={"tp": partner}, device_id_type=MESH)

    def dw_out(mb, o):
        return pltpu.make_async_copy(
            dwb.at[o], dw.at[pl.ds(pl.multiple_of(mb * mb_rows, mb_rows), mb_rows),
                             pl.ds(pl.multiple_of(o * pc, pc), pc)], dwo_sem.at[o])

    def dx_out(j):
        cols = pl.ds(pl.multiple_of(j * hb, hb), hb)
        return (pltpu.make_async_copy(dxo.at[j, pl.ds(0, rows)], dxa.at[:, cols], dxo_sem.at[j, 0]),
                pltpu.make_async_copy(dxo.at[j, pl.ds(rows, rows)], dxb.at[:, cols], dxo_sem.at[j, 1]))

    last = chips - 1
    g_steps = chips - 1
    dw_first = chips

    def scatter_step(i, carry):
        s = i // BLOCKS
        j = lax.rem(i, BLOCKS)
        k0 = pl.multiple_of(lax.rem(s + 1, chips) * slot_rows, slot_rows)
        b0 = lax.rem(s, BUFS)

        @pl.when(s >= 1)
        def _():
            for r in range(RINGS):
                rs_copy(s - 1, j, r).wait_recv()

        tile = None
        for lp in range(PIECES):
            part = lax.dot_general(
                xg[lp, pl.ds(k0, slot_rows), :],
                wv[lp // HALF, pl.ds(pl.multiple_of(j * hb, hb), hb), (lp % HALF) * pc:(lp % HALF + 1) * pc],
                (((1,), (1,)), ((), ())), preferred_element_type=F32)
            tile = part if tile is None else tile + part
        buf[b0, j] = buf[b0, j] + tile

        @pl.when(s < last)
        def _():
            @pl.when(s >= 2)
            def _():
                for r in range(RINGS):
                    pl.semaphore_wait(credit.at[j, r], 1)
            for r in range(RINGS):
                rs_copy(s, j, r).start()

        @pl.when(s == last)
        def _():
            dxo[j] = buf[b0, j].astype(BF16)
            for c in dx_out(j):
                c.start()

        @pl.when(i < g_steps)
        def _():
            nxt = lax.rem(i + 2, chips)

            def prefetch(lp):
                @pl.when(i < g_steps - 1)
                def _():
                    e_read(lax.rem(i + 3, chips), lp).start()
            form_g(nxt, prefetch)

        @pl.when((i >= dw_first) & (i < dw_first + MBLOCKS * PIECES))
        def _():
            q = i - dw_first
            mb = q // PIECES
            o = lax.rem(q, PIECES)
            lp = lax.rem(o + HALF, PIECES)

            @pl.when(o == 0)
            def _():
                xt_read(mb).wait()

                @pl.when(mb < MBLOCKS - 1)
                def _():
                    xt_read(mb + 1).start()

                @pl.when(mb >= 2)
                def _():
                    pl.semaphore_wait(dw_credit, 1)

            @pl.when((o < HALF) & (mb >= 1))
            def _():
                dw_copy(mb - 1, o).wait_send()
            stage[o] = jnp.dot(xtb[lax.rem(mb, 2)], xg[lp], preferred_element_type=F32)

            @pl.when(o < HALF)
            def _():
                dw_copy(mb, o).start()

            @pl.when(o >= HALF)
            def _():
                h = o - HALF
                dw_copy(mb, h).wait_recv()

                @pl.when(mb >= 1)
                def _():
                    dw_out(mb - 1, h).wait()
                dwb[h] = (stage[o] + dwr[lax.rem(mb, 2), h]).astype(BF16)
                dw_out(mb, h).start()

                @pl.when((h == HALF - 1) & (mb < MBLOCKS - 2))
                def _():
                    pl.semaphore_signal(dw_credit, inc=1, device_id={"tp": partner}, device_id_type=MESH)

        @pl.when(s >= 1)
        def _():
            for r in range(RINGS):
                rs_copy(s - 1, j, r).wait_send()

            @pl.when(s - 1 <= last - 3)
            def _():
                for r in range(RINGS):
                    pl.semaphore_signal(credit.at[j, r], inc=1, device_id=dev(up[r]), device_id_type=MESH)
        return carry

    lax.fori_loop(0, chips * BLOCKS, scatter_step, 0)

    ls_copy.wait()
    both = (ls_out[...] + ls_in[...]) * (1.0 / tokens)
    loss[0] = both[0, lanes - 1]
    loss[1] = both[1, lanes - 1]
    for o in range(HALF):
        dw_copy(MBLOCKS - 1, o).wait_send()
        dw_out(MBLOCKS - 1, o).wait()
    for j in range(BLOCKS):
        for c in dx_out(j):
            c.wait()


def solution(mesh):
    group = mesh.shape["tp"]
    chips = group // 2

    def local_step(x_a, x_b, labels_a, labels_b, w_local):
        rows, hidden = x_a.shape
        shard = w_local.shape[1]
        slot_rows = 2 * rows
        all_rows = chips * slot_rows
        hb = hidden // BLOCKS
        pc = shard // HALF
        mb_rows = hidden // MBLOCKS
        any_spec = pl.BlockSpec(memory_space=pl.ANY)
        vmem_spec = pl.BlockSpec(memory_space=pltpu.VMEM)
        dma = pltpu.SemaphoreType.DMA
        regular = pltpu.SemaphoreType.REGULAR
        out = pl.pallas_call(
            functools.partial(head_kernel, group),
            name="head",
            out_shape=(
                jax.ShapeDtypeStruct((2,), F32),
                jax.ShapeDtypeStruct((hidden, shard), BF16),
                jax.ShapeDtypeStruct((rows, hidden), BF16),
                jax.ShapeDtypeStruct((rows, hidden), BF16),
                jax.ShapeDtypeStruct((chips, PIECES, slot_rows, pc), F32),
                jax.ShapeDtypeStruct((hidden, all_rows), BF16),
            ),
            in_specs=[any_spec, any_spec, vmem_spec, vmem_spec, any_spec],
            out_specs=(pl.BlockSpec(memory_space=pltpu.SMEM), any_spec, any_spec, any_spec, any_spec, any_spec),
            scratch_shapes=[
                pltpu.VMEM((2, hidden, shard), BF16),
                pltpu.VMEM((PIECES, all_rows, pc), BF16),
                pltpu.VMEM((PIECES, slot_rows, pc), F32),
                pltpu.VMEM((hidden, slot_rows), BF16),
                pltpu.VMEM((2, mb_rows, all_rows), BF16),
                pltpu.VMEM((BUFS, BLOCKS, slot_rows, hb), F32),
                pltpu.VMEM((2, HALF, mb_rows, pc), F32),
                pltpu.VMEM((HALF, mb_rows, pc), BF16),
                pltpu.VMEM((BLOCKS, slot_rows, hb), BF16),
                pltpu.VMEM((all_rows, 128), F32),
                pltpu.VMEM((slot_rows, 128), F32),
                pltpu.VMEM((slot_rows, 128), F32),
                pltpu.VMEM((slot_rows, 128), jnp.int32),
                pltpu.VMEM((chips, 8, rows), F32),
                pltpu.VMEM((chips, RINGS, 8, 128), F32),
                pltpu.VMEM((chips, RINGS, 8, 128), F32),
                pltpu.VMEM((chips, 8, 128), F32),
                pltpu.VMEM((8, 128), F32),
                pltpu.VMEM((8, 128), F32),
                pltpu.VMEM((8, 128), F32),
                dma((2 * BLOCKS,)),
                dma((1,)),
                dma((2,)),
                dma((2, chips)),
                dma((4, BLOCKS * RINGS)),
                dma((chips, BLOCKS * RINGS)),
                dma((PIECES,)),
                dma((1,)),
                dma((2,)),
                dma((chips,)),
                dma((chips,)),
                dma((chips,)),
                dma((chips,)),
                dma((2,)),
                dma((BUFS, BLOCKS, RINGS)),
                dma((BUFS, BLOCKS, RINGS)),
                regular((BLOCKS, RINGS)),
                dma((HALF,)),
                dma((2, HALF)),
                regular,
                dma((HALF,)),
                dma((BLOCKS, 2)),
            ],
            compiler_params=pltpu.CompilerParams(
                collective_id=0, has_side_effects=True, vmem_limit_bytes=67043328),
        )(x_a, x_b, labels_a.reshape(1, rows), labels_b.reshape(1, rows), w_local)
        return out[0], out[1], out[2], out[3]

    row_spec = P(("dp", "tp"), None)
    label_spec = P(("dp", "tp"))
    return jax.shard_map(local_step, mesh=mesh, in_specs=(row_spec, row_spec, label_spec, label_spec, P(None, "tp")), out_specs=(P("dp"), P("dp", "tp"), row_spec, row_spec), check_vma=False)
```

time: 723 us -> 308 us (0.43)
  waiting for transfers between devices: 392 us -> 0 us
  Pallas kernels: 0 us -> 299 us
  matrix products: 182 us -> 0 us
  blocking collectives: 77.5 us -> 0 us
  other arithmetic: 53.7 us -> 0 us
  between operations: 13.8 us -> 0.64 us
    pallas_call x0 -> x1, Pallas kernels: none -> 299 us  [local_step(): pl.pallas_call(functools.partial(head_kernel, group), name='head', out_sh...]
    reduce_scatter x1 -> x0, waiting for transfers between devices: 222 us -> none  [local_step(): lax.psum_scatter(grad_part, 'tp', scatter_dimension=1, tiled=True)]
    dot_general x3 -> x0, matrix products: 182 us -> none  [the longest x1 60.8 us: local_step(): jnp.einsum('mth,hv->mtv', x_full, w_local, preferred_element_type=jnp.flo...]
    psum x1 -> x0, waiting for transfers between devices: 89.5 us -> none  [local_step(): lax.psum(jnp.stack([jnp.sum(shifted, axis=-1), local_target]), 'tp')]
    all_gather x1 -> x0, waiting for transfers between devices: 80.4 us -> none  [local_step(): x_full = lax.all_gather(jnp.stack([x_a, x_b]), 'tp', axis=1, tiled=True)]
    pmax x1 -> x0, blocking collectives: 44.8 us -> none  [local_step(): row_max = lax.pmax(jnp.max(logits, axis=-1), 'tp')]
    all_gather x1 -> x0, blocking collectives: 32.6 us -> none  [local_step(): lax.all_gather(jnp.stack([labels_a, labels_b]), 'tp', axis=1, tiled=True)]
    convert_element_type x2 -> x0, other arithmetic: 27.4 us -> none  [the longest x1 25.7 us: local_step(): ((shifted / row_sum[..., None] - label_hit.astype(jnp.float32)) / tokens)...]
  transfers between devices with their start and end apart: 3 -> 0, of which waited for: 3 -> 0; matrix products, arithmetic and copies ran while one was open for 9% -> 0% of each run, Pallas kernels for 0% -> 0%
where the time goes in v1:
time: 308 us
  Pallas kernels  299 us (97%)
  local copies, waits for them, and re-layouts  8.71 us (3%)
    pallas_call x1, Pallas kernels, local_step(): pl.pallas_call(functools.partial(head_kernel, group), name='head', out_sh...  299 us
    unnamed x8, local copies, waits for them, and re-layouts  8.71 us

profile of v1, /device:TPU:97, one launch (start us, length us, event | category | flops | bytes accessed | tf_op | source)
XLA Modules:
  0.0 308.0 jit_solution(4895670044797217234)
XLA Ops:
  0.6 298.6 %head.1 = (f32[2]{0:T(128)}, bf16[2048,1536]{1,0:T(8,128)(2,1)}, bf16[128,2048]{1,0:T(8,128)(2,1)}, bf16[128,2048]{1,0:T(8,128)(2,1)}, f32[16,6,256,512]{3,2,1,0:T(8,128)}, /*index=5*/bf16[2048,4096]{1,0:T(8,128)(2,1)}) custom-call(bf16[128,2048]{1,0:T(8,128)(2,1)} %xa.1, bf16[128,2048]{1,0:T(8,128)(2,1)} %xb.1, s32[1,128]{1,0:T(1,128)} %bitcast.2, ...), custom_call_target="tpu_custom_call" | custom-call | tf_op jit(solution)/shard_map/head/pallas_call | solution.py:513
  299.3 1.1 copy.13
  300.4 0.0 copy-start.1
  300.4 0.0 copy-start
  300.4 6.0 %copy.14 = bf16[2048,1536]{1,0:T(8,128)(2,1)} copy(bf16[2048,1536]{1,0:T(8,128)(2,1)} %get-tuple-element.17) | data formatting | bytes 12582912
  306.4 0.0 copy-done.1
  306.4 0.8 copy.15
  307.2 0.0 copy-done
  307.2 0.8 copy.16
Async XLA Ops:
  300.4 6.0 %copy-start.1 = (bf16[128,2048]{1,0:T(8,128)(2,1)S(1)}, bf16[128,2048]{1,0:T(8,128)(2,1)}, u32[]{:S(2)}) copy-start(bf16[128,2048]{1,0:T(8,128)(2,1)} %get-tuple-element.18) | copy-start | bytes 1572868
  300.4 6.8 %copy-start = (bf16[128,2048]{1,0:T(8,128)(2,1)S(1)}, bf16[128,2048]{1,0:T(8,128)(2,1)}, u32[]{:S(2)}) copy-start(bf16[128,2048]{1,0:T(8,128)(2,1)} %get-tuple-element.19) | copy-start | bytes 1572868
